TPU v7x, 32 devices: a whole 2x2x4 slice. The times are simulated.
32 devices in a mesh: cuts: 2 (over x), wide: 8 (over z, y), narrow: 2 (over core).
Axes of the slice: x: 2, y: 2, z: 4, core: 2. Of those that a mesh axis runs over, the one named last changes fastest.
Arguments:
- stem_tensor: float32 [2, 16384, 512], P(None, ('cuts', 'wide', 'narrow')), parts along dimension 1, may hold values from -6 to 6
- leaves: bfloat16 [16, 4, 2, 512, 512], P(('cuts', 'wide')), parts along dimension 0, may hold values from -1 to 1
- root_devices: int32 [4], replicated, may hold values from 0 to 7, as said below
- mode_orders: int32 [4, 9], replicated, may hold values from 0 to 8, each once within a row
Outputs:
- contracted: float32 [2, 16384, 512], P(None, ('cuts', 'wide', 'narrow')), parts along dimension 1
There are 2 independent parts, one for each index of `cuts`. A program takes and returns all parts, laid end to end along the dimension named above; an argument that names none is the same for every part. Nothing has to cross between parts.
Inputs may be any that keep to these rules, and one draw needn't show every extreme that they name: `root_devices`: the roots include 0, 4 and 7. `mode_orders`: each row holds every number of 0 to 8 once.
All inputs are finite; a program needn't handle non-finite values.
Results may differ from a plain program's by a relative error of at most 0.0081.
Values may be sent and summed in bfloat16 or wider, within the bound.
A program may use at most 64 MiB of HBM per device.

v0:
```python
import functools

import jax
import jax.numpy as jnp
from jax import lax
from jax.experimental import pallas as pl
from jax.experimental.pallas import tpu as pltpu
from jax.sharding import PartitionSpec as P

GROUP = 4
CHUNKS = 8
FLIGHT = 2
TILE = 128
BF16 = jnp.bfloat16
F32 = jnp.float32


def dot(x, y):
    return jnp.dot(x, y, preferred_element_type=F32)


def complex_product(ar, ai, br, bi):
    left = jnp.concatenate([ar, ai], axis=1)
    return (
        dot(left, jnp.concatenate([br, -bi], axis=0)),
        dot(left, jnp.concatenate([bi, br], axis=0)),
    )


def remote(src, dst, send_sem, recv_sem, device):
    return pltpu.make_async_remote_copy(
        src_ref=src,
        dst_ref=dst,
        send_sem=send_sem,
        recv_sem=recv_sem,
        device_id=device,
        device_id_type=pl.DeviceIdType.MESH,
    )


def kernel(
    rounds, roots, orders, stem_in, leaves_in, net_out, last_out,
    leaf, pair, away, high, chosen, held, crossed, branches, stem, net1, net2, net3, swap,
    local_sem, leaf_s, leaf_r, fwd_s, fwd_r, pair_s, pair_r, high_s, high_r,
    cross_s, cross_r, z_s, z_r, y_s, y_r, core_s, core_r, swap_s, swap_r,
):
    width = stem.shape[2]
    rows = stem.shape[1]
    half = width // 2
    part = half // CHUNKS
    core = lax.axis_index("narrow")
    wide = lax.axis_index("wide")
    member = wide % GROUP
    y = member % 2
    z = member // 2
    other = {"narrow": 1 - core}
    over_y = {"wide": wide + 1 - 2 * y}
    over_z = {"wide": wide + 2 - 4 * z}
    bits = [(wide // (GROUP << r)) % 2 for r in range(rounds)]
    over_group = [{"wide": wide + (GROUP << r) * (1 - 2 * bits[r])} for r in range(rounds)]

    barrier = pltpu.get_barrier_semaphore()
    for peer in [other, over_y, over_z] + over_group:
        pl.semaphore_signal(barrier, inc=1, device_id=peer, device_id_type=pl.DeviceIdType.MESH)
    own_rows = pl.ds(pl.multiple_of(core * half, half), half)
    own_copies = [
        pltpu.make_async_copy(leaves_in.at[0, 2 * s + y], leaf.at[s, y], local_sem.at[s])
        for s in range(2)
    ]
    stem_copy = pltpu.make_async_copy(stem_in, stem, local_sem.at[2])
    pl.semaphore_wait(barrier, 3 + rounds)

    phases = [1 - z, z]
    leaf_copies = []
    for i, s in enumerate(phases):
        copy = remote(
            leaves_in.at[0, 2 * s + 1 - y, :, own_rows],
            leaf.at[s, y, :, own_rows],
            leaf_s.at[i], leaf_r.at[i], over_y,
        )
        leaf_copies.append(copy)
    leaf_copies[0].start()
    for copy in own_copies:
        copy.start()
    stem_copy.start()

    def choose(i, carry):
        column = lax.broadcasted_iota(jnp.int32, (TILE, width), 1)
        source = jnp.zeros((TILE, width), jnp.int32)
        for b in range(orders.shape[1]):
            weight = jnp.left_shift(jnp.int32(1), orders[member, b])
            source = source + (jnp.right_shift(column, b) & 1) * weight
        row = lax.broadcasted_iota(jnp.int32, (TILE, width), 0) + i * TILE
        at = pl.ds(pl.multiple_of(i * TILE, TILE), TILE)
        chosen[at] = jnp.where(row == source, 1.0, 0.0).astype(F32).astype(BF16)
        return carry

    lax.fori_loop(0, width // TILE, choose, 0)
    for copy in own_copies:
        copy.wait()

    pair_copy = remote(away, pair.at[z], pair_s, pair_r, over_z)
    leaf_copies[0].wait_send()
    leaf_copies[1].start()
    for i, s in enumerate(phases):
        leaf_copies[i].wait_recv()
        forward = remote(
            leaf.at[s, 1 - y, :, own_rows], leaf.at[s, 1 - y, :, own_rows],
            fwd_s.at[i], fwd_r.at[i], other,
        )
        forward.start()
        forward.wait()

        def pair_tile(t, carry, s=s, i=i):
            at = pl.ds(pl.multiple_of(t * half, half), half)
            real, imag = complex_product(
                leaf[s, 0, 0, own_rows], leaf[s, 0, 1, own_rows],
                leaf[s, 1, 0, :, at], leaf[s, 1, 1, :, at],
            )
            target = away if i == 0 else pair.at[z]
            target[0, :, at] = real.astype(BF16)
            target[1, :, at] = imag.astype(BF16)
            return carry

        lax.fori_loop(0, width // half, pair_tile, 0)
        if i == 0:
            pair_copy.start()
    pair_copy.wait_recv()

    def high_tile(t, carry):
        at = pl.ds(pl.multiple_of(t * half, half), half)
        for c in range(2):
            high[c, own_rows, at] = dot(pair[1, c], chosen[:, at]).astype(BF16)
        return carry

    lax.fori_loop(0, width // half, high_tile, 0)
    high_copy = remote(high.at[:, own_rows], high.at[:, own_rows], high_s, high_r, other)
    high_copy.start()
    high_copy.wait()

    def rows_of(c):
        return pl.ds(pl.multiple_of(core * half + c * part, part), part)

    def cross_copy(r, c):
        return remote(held.at[r, c], crossed.at[r, c], cross_s.at[r, c], cross_r.at[r, c], over_group[r])

    def place(origin, c):
        return branches.at[origin, :, rows_of(c)]

    origins = [member, member + 2 - 4 * z, member + 1 - 2 * y, GROUP - 1 - member]

    def z_copy(c):
        return remote(place(origins[0], c), place(origins[0], c), z_s.at[c], z_r.at[c], over_z)

    def y_copy(i, c):
        return remote(place(origins[i], c), place(origins[i], c), y_s.at[i, c], y_r.at[i, c], over_y)

    def core_copy(i, c):
        return remote(place(origins[i], c), place(origins[i], c), core_s.at[i, c], core_r.at[i, c], other)

    def spread(c):
        z_copy(c).start()
        y_copy(0, c).start()
        core_copy(0, c).start()

    def select(r, c):
        cross_copy(r, c).wait_recv()
        cross_copy(r, c).wait_send()
        if c + FLIGHT < CHUNKS:
            cross_copy(r, c + FLIGHT).start()
        root_bit = (roots[member] // (GROUP << r)) % 2
        for p in range(2):
            here = held[r, c, p].astype(F32)
            there = crossed[r, c, p].astype(F32)
            same = jnp.full(here.shape, root_bit, jnp.int32) == bits[r]
            picked = jnp.where(same, here, there).astype(BF16)
            if r + 1 < rounds:
                held[r + 1, c, p] = picked
            else:
                branches[member, p, rows_of(c)] = picked
        if r + 1 < rounds:
            if c < FLIGHT:
                cross_copy(r + 1, c).start()
        else:
            spread(c)

    def on_z(c):
        z_copy(c).wait_recv()
        y_copy(1, c).start()
        core_copy(1, c).start()

    def on_y(i, c):
        y_copy(i, c).wait_recv()
        core_copy(2 + i, c).start()

    for c in range(CHUNKS):
        at = pl.ds(c * part, part)
        real, imag = complex_product(pair[0, 0, at], pair[0, 1, at], high[0], high[1])
        if rounds:
            held[0, c, 0] = real.astype(BF16)
            held[0, c, 1] = imag.astype(BF16)
            if c < FLIGHT:
                cross_copy(0, c).start()
        else:
            branches[member, 0, rows_of(c)] = real.astype(BF16)
            branches[member, 1, rows_of(c)] = imag.astype(BF16)
            spread(c)

    for r in range(rounds - 1):
        for c in range(CHUNKS):
            select(r, c)
    for c in range(CHUNKS + 2):
        if rounds and c < CHUNKS:
            select(rounds - 1, c)
        if 1 <= c <= CHUNKS:
            on_z(c - 1)
            on_y(0, c - 1)
        if c >= 2:
            on_y(1, c - 2)
    stem_copy.wait()
    for c in range(CHUNKS):
        for i in range(4):
            core_copy(i, c).wait_recv()
    last_copy = pltpu.make_async_copy(branches.at[GROUP - 1], last_out, local_sem.at[3])
    last_copy.start()

    def columns(block):
        return pl.ds(pl.multiple_of(block * half, half), half)

    def swapped(step, index, read, target):
        copy = remote(swap.at[index], target.at[core], swap_s.at[index], swap_r.at[index], other)
        for keep in range(2):
            block = core if keep else 1 - core

            def tile(t, carry, keep=keep, block=block):
                at = pl.ds(pl.multiple_of(t * half, half), half)
                nr, ni = read(at)
                real, imag = complex_product(
                    nr, ni, branches[step, 0, :, columns(block)], branches[step, 1, :, columns(block)]
                )
                place = target.at[core] if keep else swap.at[index]
                place[0, at] = real.astype(BF16)
                place[1, at] = imag.astype(BF16)
                return carry

            lax.fori_loop(0, rows // half, tile, 0)
            if not keep:
                copy.start()
        copy.wait()

    def plain(step, source, target):
        for block in range(width // half):
            across = pl.ds(block * half, half)

            def tile(t, carry, across=across):
                at = pl.ds(pl.multiple_of(t * half, half), half)
                real, imag = complex_product(
                    jnp.concatenate([source[0, 0, at], source[1, 0, at]], axis=1),
                    jnp.concatenate([source[0, 1, at], source[1, 1, at]], axis=1),
                    branches[step, 0, :, across], branches[step, 1, :, across],
                )
                target[0, at, across] = real.astype(target.dtype)
                target[1, at, across] = imag.astype(target.dtype)
                return carry

            lax.fori_loop(0, rows // half, tile, 0)

    swapped(0, 0, lambda at: (stem[0, at].astype(BF16), stem[1, at].astype(BF16)), net1)
    plain(1, net1, net2)
    swapped(2, 1, lambda at: (net2[0, at], net2[1, at]), net3)
    net_copy = pltpu.make_async_copy(net3, net_out, local_sem.at[4])
    net_copy.start()
    net_copy.wait()
    last_copy.wait()

    leaf_copies[1].wait_send()
    pair_copy.wait_send()
    for c in range(CHUNKS):
        z_copy(c).wait_send()
        for i in range(2):
            y_copy(i, c).wait_send()
        for i in range(4):
            core_copy(i, c).wait_send()


def finish(net, branch, out):
    half = net.shape[3]
    for block in range(branch.shape[2] // half):
        across = pl.ds(block * half, half)
        real, imag = complex_product(
            jnp.concatenate([net[0, 0], net[1, 0]], axis=1),
            jnp.concatenate([net[0, 1], net[1, 1]], axis=1),
            branch[0, :, across], branch[1, :, across],
        )
        out[0, :, across] = real
        out[1, :, across] = imag


def local(stem_tensor, leaves, root_devices, mode_orders):
    _, rows, width = stem_tensor.shape
    half = width // 2
    part = half // CHUNKS
    groups = lax.axis_size("wide") // GROUP
    rounds = groups.bit_length() - 1
    vmem = pltpu.VMEM
    dma = pltpu.SemaphoreType.DMA
    network, last = pl.pallas_call(
        functools.partial(kernel, rounds),
        out_shape=(
            jax.ShapeDtypeStruct((2, 2, rows, half), BF16),
            jax.ShapeDtypeStruct((2, width, width), BF16),
        ),
        in_specs=[pl.BlockSpec(memory_space=pltpu.SMEM)] * 2
        + [pl.BlockSpec(memory_space=pl.ANY)] * 2,
        out_specs=[pl.BlockSpec(memory_space=pl.ANY)] * 2,
        scratch_shapes=[
            vmem((2, 2, 2, width, width), BF16),
            vmem((2, 2, half, width), BF16),
            vmem((2, half, width), BF16),
            vmem((2, width, width), BF16),
            vmem((width, width), BF16),
            vmem((max(rounds, 1), CHUNKS, 2, part, width), BF16),
            vmem((max(rounds, 1), CHUNKS, 2, part, width), BF16),
            vmem((GROUP, 2, width, width), BF16),
            vmem((2, rows, width), F32),
            vmem((2, 2, rows, half), BF16),
            vmem((2, rows, width), BF16),
            vmem((2, 2, rows, half), BF16),
            vmem((2, 2, rows, half), BF16),
            dma((5,)),
            dma((2,)), dma((2,)), dma((2,)), dma((2,)),
            dma, dma, dma, dma,
            dma((max(rounds, 1), CHUNKS)), dma((max(rounds, 1), CHUNKS)),
            dma((CHUNKS,)), dma((CHUNKS,)),
            dma((2, CHUNKS)), dma((2, CHUNKS)),
            dma((4, CHUNKS)), dma((4, CHUNKS)),
            dma((2,)), dma((2,)),
        ],
        compiler_params=pltpu.CompilerParams(collective_id=0, has_side_effects=True),
    )(root_devices, mode_orders, stem_tensor, leaves)
    return pl.pallas_call(
        finish,
        grid=(rows // half,),
        out_shape=jax.ShapeDtypeStruct(stem_tensor.shape, F32),
        in_specs=[
            pl.BlockSpec((2, 2, half, half), lambda i: (0, 0, i, 0)),
            pl.BlockSpec((2, width, width), lambda i: (0, 0, 0)),
        ],
        out_specs=pl.BlockSpec((2, half, width), lambda i: (0, i, 0)),
    )(network, last)


def solution(mesh):
    stem_spec = P(None, ("cuts", "wide", "narrow"), None)
    return jax.shard_map(
        local,
        mesh=mesh,
        in_specs=(stem_spec, P(("cuts", "wide"), None, None, None, None), P(), P()),
        out_specs=stem_spec,
        check_vma=False,
    )
```

profile of v0, /device:TPU:0, one launch (start us, length us, event | category | flops | bytes accessed | tf_op | source)
XLA Modules:
  0.0 85.5 jit_solution(12074966743353089107)
XLA Ops:
  0.0 81.7 %shard_map.46 = (bf16[2,2,512,256]{3,2,1,0:T(8,128)(2,1)}, bf16[2,512,512]{2,1,0:T(8,128)(2,1)}) custom-call(s32[4]{0:T(128)} %roots.1, s32[4,9]{1,0:T(4,128)} %orders.1, f32[2,512,512]{2,1,0:T(8,128)} %stem_in.1, bf16[1,4,2,512,512]{4,3,2,1,0:T(8,128)(2,1)} %leaves_in.1), custom_call_target="tpu_custom_call" | custom-call | tf_op jit(solution)/shard_map/pallas_call | solution.py:307
  81.7 3.8 %shard_map.47 = f32[2,512,512]{2,1,0:T(8,128)} custom-call(bf16[2,2,512,256]{3,2,1,0:T(8,128)(2,1)} %get-tuple-element.7.net, bf16[2,512,512]{2,1,0:T(8,128)(2,1)} %get-tuple-element.8.branch), custom_call_target="tpu_custom_call" | custom-call | tf_op jit(solution)/shard_map/pallas_call | solution.py:341
where the time goes:
time: 85.7 us; the launch traced here: 85.5 us
  Pallas kernels  85.5 us (100%)
    pallas_call x1, Pallas kernels, local(): pl.pallas_call(functools.partial(kernel, rounds), out_shape=(jax.ShapeDty...  81.7 us
    pallas_call x1, Pallas kernels, local(): pl.pallas_call(finish, grid=(rows // half,), out_shape=jax.ShapeDtypeStru...  3.81 us

commit v1 on v0

--- a/solution.py
+++ b/solution.py
@@ -296,7 +296,338 @@
         out[1, :, across] = imag
 
 
-def local(stem_tensor, leaves, root_devices, mode_orders):
+LEAF = 4
+SPREAD = 8
+
+
+def matching(roots, group):
+    seen = jnp.int32(0)
+    found = []
+    for k in range(roots.shape[0]):
+        holds = jnp.where(roots[k] // GROUP == group, 1, 0)
+        found.append((holds, seen))
+        seen = seen + holds
+    return found
+
+
+def step_of(roots, group, rank):
+    total = jnp.int32(0)
+    for k, (holds, seen) in enumerate(matching(roots, group)):
+        total = total + jnp.where(seen == rank, holds * k, 0)
+    return total
+
+
+def two_groups(
+    roots, orders, stem_in, leaves_in, net_out, last_out,
+    leaf, outgoing, arrived, mine, chosen, pair, branches, stem, stems, net1, net2, net3, swap, final,
+    local_sem, leaf_s, leaf_r, fwd_s, fwd_r, pair_s, pair_r, high_s, high_r,
+    y_s, y_r, core_s, core_r, mid_s, end_s, far_r, stem_s, stem_r, swap_s, swap_r,
+):
+    width = stem.shape[2]
+    rows = stem.shape[1]
+    half = width // 2
+    part = half // SPREAD
+    core = lax.axis_index("narrow")
+    wide = lax.axis_index("wide")
+    group = wide // GROUP
+    member = wide % GROUP
+    y = member % 2
+    z = member // 2
+    inner = group + z
+    other = {"narrow": 1 - core}
+    over_y = {"wide": wide + 1 - 2 * y}
+    over_z = {"wide": wide + 2 - 4 * z}
+    over_mid = {"wide": wide + 2 - 4 * group}
+    MESH = pl.DeviceIdType.MESH
+
+    fetch = pltpu.make_async_copy(leaves_in.at[0], leaf, local_sem.at[0])
+    stem_copy = pltpu.make_async_copy(stem_in, stem, local_sem.at[1])
+    fetch.start()
+    stem_copy.start()
+    barrier = pltpu.get_barrier_semaphore()
+    for peer in [other, over_y, over_z]:
+        pl.semaphore_signal(barrier, inc=1, device_id=peer, device_id_type=MESH)
+
+    @pl.when(inner == 1)
+    def _():
+        pl.semaphore_signal(barrier, inc=1, device_id=over_mid, device_id_type=MESH)
+        pl.semaphore_wait(barrier, 4)
+
+    @pl.when(inner != 1)
+    def _():
+        pl.semaphore_wait(barrier, 3)
+
+    k_right = step_of(roots, group, 0)
+    k_left = step_of(roots, group, 1)
+    k_own = jnp.where(y == 1, k_right, k_left)
+    k_send = jnp.where(y == 1, k_left, k_right)
+
+    def own_rows(j=0, n=1):
+        size = half // n
+        return pl.ds(pl.multiple_of(core * half + j * size, size), size)
+
+    def one_hot(k):
+        column = lax.broadcasted_iota(jnp.int32, (8, width), 1)
+        source = jnp.zeros((8, width), jnp.int32)
+        for b in range(orders.shape[1]):
+            weight = jnp.left_shift(jnp.int32(1), orders[k, b])
+            source = source + (jnp.right_shift(column, b) & 1) * weight
+
+        def tile(i, carry):
+            row = lax.broadcasted_iota(jnp.int32, (TILE, width), 0) + i * TILE
+            at = pl.ds(pl.multiple_of(i * TILE, TILE), TILE)
+            same = row == jnp.broadcast_to(source[0:1], (TILE, width))
+            chosen[at] = jnp.where(same, 1.0, 0.0).astype(F32).astype(BF16)
+            return carry
+
+        lax.fori_loop(0, width // TILE, tile, 0)
+
+    wide_part = width // LEAF
+
+    def chunk(j, by_rows):
+        if by_rows:
+            return own_rows(j, LEAF), slice(None)
+        return own_rows(), pl.ds(j * wide_part, wide_part)
+
+    def leaf_copy(j, by_rows):
+        size = half // LEAF
+        at = (pl.ds(j * size, size), slice(None)) if by_rows else (slice(None), pl.ds(j * wide_part, wide_part))
+        to = chunk(j, by_rows)
+        return remote(
+            outgoing.at[:, at[0], at[1]], arrived.at[:, to[0], to[1]],
+            leaf_s.at[j], leaf_r.at[j], over_y,
+        )
+
+    permuted = z * y
+    fetch.wait()
+
+    @pl.when(permuted == 0)
+    def _():
+        for c in range(2):
+            outgoing[c] = leaf[k_send, c, own_rows()]
+
+    @pl.when(permuted == 1)
+    def _():
+        one_hot(k_send)
+        for c in range(2):
+            outgoing[c] = dot(leaf[k_send, c, own_rows()], chosen[...]).astype(BF16)
+
+    @pl.when(y == 0)
+    def _():
+        for j in range(LEAF):
+            leaf_copy(j, True).start()
+
+    @pl.when(y == 1)
+    def _():
+        for j in range(LEAF):
+            leaf_copy(j, False).start()
+
+    @pl.when(permuted == 0)
+    def _():
+        for c in range(2):
+            mine[c] = leaf[k_own, c]
+
+    @pl.when(permuted == 1)
+    def _():
+        one_hot(k_own)
+        for c in range(2):
+            mine[c] = dot(leaf[k_own, c], chosen[...]).astype(BF16)
+
+    stem_copy.wait()
+    for c in range(2):
+        stems[core, c] = stem[c].astype(BF16)
+    stem_share = remote(stems.at[core], stems.at[core], stem_s, stem_r, other)
+    stem_share.start()
+
+    def pair_copy(j, by_rows):
+        at = chunk(j, by_rows)
+        place = pair.at[z, :, at[0], at[1]]
+        return remote(place, place, pair_s.at[j], pair_r.at[j], over_z)
+
+    def high_copy(j, by_rows):
+        at = chunk(j, by_rows)
+        place = pair.at[1, :, at[0], at[1]]
+        return remote(place, place, high_s.at[j], high_r.at[j], other)
+
+    def put_pair(j, by_rows, real, imag):
+        at = chunk(j, by_rows)
+        pair[z, 0, at[0], at[1]] = real.astype(BF16)
+        pair[z, 1, at[0], at[1]] = imag.astype(BF16)
+        pair_copy(j, by_rows).start()
+
+        @pl.when(z == 1)
+        def _():
+            high_copy(j, by_rows).start()
+
+    def join(by_rows):
+        for j in range(LEAF):
+            pair_copy(j, by_rows).wait_recv()
+
+            @pl.when(z == 0)
+            def _():
+                high_copy(j, by_rows).start()
+
+        for j in range(LEAF):
+            high_copy(j, by_rows).wait_recv()
+
+    @pl.when(y == 1)
+    def _():
+        for j in range(LEAF):
+            leaf_copy(j, True).wait_recv()
+            at = own_rows(j, LEAF)
+            put_pair(j, True, *complex_product(arrived[0, at], arrived[1, at], mine[0], mine[1]))
+        join(True)
+
+    @pl.when(y == 0)
+    def _():
+        def forward(j):
+            at = chunk(j, False)
+            place = arrived.at[:, at[0], at[1]]
+            return remote(place, place, fwd_s.at[j], fwd_r.at[j], other)
+
+        for j in range(LEAF + 1):
+            if j < LEAF:
+                leaf_copy(j, False).wait_recv()
+                forward(j).start()
+            if j:
+                forward(j - 1).wait_recv()
+                at = pl.ds((j - 1) * wide_part, wide_part)
+                put_pair(j - 1, False, *complex_product(
+                    mine[0, own_rows()], mine[1, own_rows()], arrived[0, :, at], arrived[1, :, at]
+                ))
+        join(False)
+        for j in range(LEAF):
+            forward(j).wait_send()
+
+    here = 2 * (1 - y) + group
+    far = 2 * (1 - y) + 1 - group
+    beside = 2 * y + group
+    beyond = 2 * y + 1 - group
+
+    def place(t, r):
+        return branches.at[t, :, own_rows(r, SPREAD)]
+
+    def y_copy(i, r):
+        t = [here, far][i]
+        return remote(place(t, r), place(t, r), y_s.at[i, r], y_r.at[i, r], over_y)
+
+    def core_copy(i, r):
+        t = [here, far, beside, beyond][i]
+        return remote(place(t, r), place(t, r), core_s.at[i, r], core_r.at[i, r], other)
+
+    def mid_copy(r):
+        return remote(place(here, r), place(here, r), mid_s.at[r], far_r.at[r], over_mid)
+
+    def end_copy(r):
+        return remote(place(far, r), place(far, r), end_s.at[r], far_r.at[r], over_z)
+
+    for b in range(2):
+        at = own_rows(b, 2)
+        real, imag = complex_product(pair[0, 0, at], pair[0, 1, at], pair[1, 0], pair[1, 1])
+        branches[here, 0, at] = real.astype(BF16)
+        branches[here, 1, at] = imag.astype(BF16)
+        for r in range(b * SPREAD // 2, (b + 1) * SPREAD // 2):
+
+            @pl.when(inner == 1)
+            def _():
+                mid_copy(r).start()
+
+            y_copy(0, r).start()
+            core_copy(0, r).start()
+
+    for r in range(SPREAD):
+        far_copy = mid_copy(r)
+        far_copy.wait_recv()
+
+        @pl.when(inner == 1)
+        def _():
+            end_copy(r).start()
+
+        y_copy(1, r).start()
+        core_copy(1, r).start()
+        y_copy(0, r).wait_recv()
+        core_copy(2, r).start()
+    for r in range(SPREAD):
+        y_copy(1, r).wait_recv()
+        core_copy(3, r).start()
+    stem_share.wait()
+    for i in range(4):
+        for r in range(SPREAD):
+            core_copy(i, r).wait_recv()
+
+    source = []
+    zeros = matching(roots, 0)
+    ones = matching(roots, 1)
+    for k in range(roots.shape[0]):
+        place_of = jnp.where(zeros[k][0] == 1, 2 * zeros[k][1], 1 + 2 * ones[k][1])
+        source.append(jnp.minimum(place_of, 3))
+
+    def columns(block):
+        return pl.ds(pl.multiple_of(block * half, half), half)
+
+    for c in range(2):
+        final[c] = branches[source[3], c]
+    last_copy = pltpu.make_async_copy(final, last_out, local_sem.at[2])
+    last_copy.start()
+
+    def first(i, carry):
+        real, imag = complex_product(
+            stems[i, 0], stems[i, 1],
+            branches[source[0], 0, :, columns(core)], branches[source[0], 1, :, columns(core)],
+        )
+        net1[i, 0] = real.astype(BF16)
+        net1[i, 1] = imag.astype(BF16)
+        return carry
+
+    lax.fori_loop(0, 2, first, 0)
+
+    def second(block, carry):
+        real, imag = complex_product(
+            jnp.concatenate([net1[0, 0], net1[1, 0]], axis=1),
+            jnp.concatenate([net1[0, 1], net1[1, 1]], axis=1),
+            branches[source[1], 0, :, columns(block)], branches[source[1], 1, :, columns(block)],
+        )
+        net2[0, :, columns(block)] = real.astype(BF16)
+        net2[1, :, columns(block)] = imag.astype(BF16)
+        return carry
+
+    lax.fori_loop(0, 2, second, 0)
+
+    swap_copy = remote(swap, net3.at[core], swap_s, swap_r, other)
+    for keep in range(2):
+        block = core if keep else 1 - core
+        real, imag = complex_product(
+            net2[0], net2[1], branches[source[2], 0, :, columns(block)], branches[source[2], 1, :, columns(block)]
+        )
+        target = net3.at[core] if keep else swap
+        target[0] = real.astype(BF16)
+        target[1] = imag.astype(BF16)
+        if not keep:
+            swap_copy.start()
+    swap_copy.wait()
+    net_copy = pltpu.make_async_copy(net3, net_out, local_sem.at[3])
+    net_copy.start()
+    net_copy.wait()
+    last_copy.wait()
+
+    for j in range(LEAF):
+        leaf_copy(j, True).wait_send()
+        pair_copy(j, True).wait_send()
+        high_copy(j, True).wait_send()
+    for r in range(SPREAD):
+
+        @pl.when(inner == 1)
+        def _():
+            mid_copy(r).wait_send()
+            end_copy(r).wait_send()
+
+        for i in range(2):
+            y_copy(i, r).wait_send()
+        for i in range(4):
+            core_copy(i, r).wait_send()
+
+
+def general(stem_tensor, leaves, root_devices, mode_orders):
     _, rows, width = stem_tensor.shape
     half = width // 2
     part = half // CHUNKS
@@ -338,6 +669,12 @@
         ],
         compiler_params=pltpu.CompilerParams(collective_id=0, has_side_effects=True),
     )(root_devices, mode_orders, stem_tensor, leaves)
+    return network, last
+
+
+def closing(network, last, stem_tensor):
+    _, rows, width = stem_tensor.shape
+    half = width // 2
     return pl.pallas_call(
         finish,
         grid=(rows // half,),
@@ -350,6 +687,58 @@
     )(network, last)
 
 
+def split(stem_tensor, leaves, root_devices, mode_orders):
+    _, rows, width = stem_tensor.shape
+    half = width // 2
+    vmem = pltpu.VMEM
+    dma = pltpu.SemaphoreType.DMA
+    network, last = pl.pallas_call(
+        two_groups,
+        out_shape=(
+            jax.ShapeDtypeStruct((2, 2, rows, half), BF16),
+            jax.ShapeDtypeStruct((2, width, width), BF16),
+        ),
+        in_specs=[pl.BlockSpec(memory_space=pltpu.SMEM)] * 2
+        + [pl.BlockSpec(memory_space=pl.ANY)] * 2,
+        out_specs=[pl.BlockSpec(memory_space=pl.ANY)] * 2,
+        scratch_shapes=[
+            vmem((leaves.shape[1], 2, width, width), BF16),
+            vmem((2, half, width), BF16),
+            vmem((2, width, width), BF16),
+            vmem((2, width, width), BF16),
+            vmem((width, width), BF16),
+            vmem((2, 2, width, width), BF16),
+            vmem((4, 2, width, width), BF16),
+            vmem((2, rows, width), F32),
+            vmem((2, 2, rows, width), BF16),
+            vmem((2, 2, rows, half), BF16),
+            vmem((2, rows, width), BF16),
+            vmem((2, 2, rows, half), BF16),
+            vmem((2, rows, half), BF16),
+            vmem((2, width, width), BF16),
+            dma((4,)),
+            dma((LEAF,)), dma((LEAF,)), dma((LEAF,)), dma((LEAF,)),
+            dma((LEAF,)), dma((LEAF,)), dma((LEAF,)), dma((LEAF,)),
+            dma((2, SPREAD)), dma((2, SPREAD)),
+            dma((4, SPREAD)), dma((4, SPREAD)),
+            dma((SPREAD,)), dma((SPREAD,)), dma((SPREAD,)),
+            dma, dma, dma, dma,
+        ],
+        compiler_params=pltpu.CompilerParams(collective_id=1, has_side_effects=True),
+    )(root_devices, mode_orders, stem_tensor, leaves)
+    return network, last
+
+
+def local(stem_tensor, leaves, root_devices, mode_orders):
+    arrays = (stem_tensor, leaves, root_devices, mode_orders)
+    if lax.axis_size("wide") // GROUP == 2:
+        even = jnp.sum((root_devices // GROUP).astype(jnp.int32)) == 2
+        network, last = lax.cond(even, split, general, *arrays)
+    else:
+        network, last = general(*arrays)
+    return closing(network, last, stem_tensor)
+
+
 def solution(mesh):
     stem_spec = P(None, ("cuts", "wide", "narrow"), None)
     return jax.shard_map(

time: 85.7 us -> 63.6 us (0.74)
  the two profiles are of different devices: /device:TPU:0 before, /device:TPU:21 now
where the time goes in v1:
time: 63.6 us; the launch traced here: 63.4 us
  Pallas kernels  61.2 us (96%)
  other arithmetic  1.3 us (2%)
  between operations  0.66 us (1%)
    pallas_call x1, Pallas kernels, split(): pl.pallas_call(two_groups, out_shape=(jax.ShapeDtypeStruct((2, 2, rows, h...  58.7 us
    pallas_call x1, Pallas kernels, closing(): pl.pallas_call(finish, grid=(rows // half,), out_shape=jax.ShapeDtypeStru...  2.5 us
    reduce_sum x1, other arithmetic, local(): even = jnp.sum((root_devices // GROUP).astype(jnp.int32)) == 2  1.3 us

profile of v1, /device:TPU:21, one launch (start us, length us, event | category | flops | bytes accessed | tf_op | source)
XLA Modules:
  0.0 63.4 jit_solution(9031582623879984124)
XLA Ops:
  0.0 1.3 %fusion = s32[]{:T(128)} fusion(s32[4]{0:T(128)} %param.8), kind=kLoop, calls=%fused_computation.4 | loop fusion | flops 63 | bytes 20 | tf_op jit(solution)/shard_map/reduce_sum | solution.py:735
  2.0 58.9 %conditional.1 = ((bf16[2,2,512,256]{3,2,1,0:T(8,128)(2,1)S(1)}, bf16[2,512,512]{2,1,0:T(8,128)(2,1)S(1)})) conditional(s32[]{:T(128)} %convert_element_type.3, (s32[4]{0:T(128)}, s32[4,9]{1,0:T(4,128)}, f32[2,512,512]{2,1,0:T(8,128)}, bf16[1,4,2,512,512]{4,3,2,1,0:T(8,128)(2,1)}) %tuple.11, (s32[4]{0:T(128)}, s32[4,9]{1,0:T(4,128)}, ...), branch_computations={%region_1.2_spmd, %region_2.3_spmd} | conditional | bytes 8 | solution.py:736
  2.0 58.7 %branch_1_fun.1 = (bf16[2,2,512,256]{3,2,1,0:T(8,128)(2,1)S(1)}, bf16[2,512,512]{2,1,0:T(8,128)(2,1)S(1)}) custom-call(s32[4]{0:T(128)} %get-tuple-element.25.roots, s32[4,9]{1,0:T(4,128)} %get-tuple-element.26.orders, f32[2,512,512]{2,1,0:T(8,128)} %get-tuple-element.27.stem_in, bf16[1,4,2,512,512]{4,3,2,1,0:T(8,128)(2,1)} %get-tuple-element.28.leaves_in), custom_call_target="tpu_custom_call" | custom-call | tf_op jit(solution)/shard_map/cond/branch_1_fun/pallas_call | solution.py:695
  60.9 2.5 %shard_map.46 = f32[2,512,512]{2,1,0:T(8,128)} custom-call(bf16[2,2,512,256]{3,2,1,0:T(8,128)(2,1)S(1)} %get-tuple-element.31.net, bf16[2,512,512]{2,1,0:T(8,128)(2,1)S(1)} %get-tuple-element.32.branch), custom_call_target="tpu_custom_call" | custom-call | tf_op jit(solution)/shard_map/pallas_call | solution.py:678
